TPU v7x, 32 devices: a whole 2x2x4 slice. The times are simulated.
32 devices in a mesh: role: 4 (over z), tp: 4 (over y, x), dp: 2 (over core).
Axes of the slice: x: 2, y: 2, z: 4, core: 2. Of those that a mesh axis runs over, the one named last changes fastest.
Arguments:
- master: float32 [1024, 8192], P('tp', ('role', 'dp')), may hold values from -0.0625 to 0.0625
- key_bias: float32 [1024], P('tp'), may hold values from -3 to 3
- probe_tokens: bfloat16 [2048, 8192], P(('role', 'dp')), may hold values from -6 to 6
Outputs:
- weight: bfloat16 [8192, 1024], P(None, 'tp')
- probe_keys: bfloat16 [2048, 1024], P(('role', 'dp'), 'tp')
- checksum: float32 [8192], replicated
All inputs are finite; a program needn't handle non-finite values.
Results may differ from a plain program's by a relative error of at most 0.005.
Values may be sent and summed in bfloat16 or wider, within the bound.
A program may use at most 64 MiB of HBM per device.

v0:
```python
import jax
import jax.numpy as jnp
from jax import lax
from jax.sharding import PartitionSpec as P


def body(master, key_bias, probe_tokens):
    own_rows = jnp.transpose(master).astype(jnp.bfloat16)
    incoming = lax.all_gather(own_rows, ("role", "dp"), axis=0, tiled=True)
    totals = jnp.dot(probe_tokens, incoming, preferred_element_type=jnp.float32)
    probe_keys = (totals + key_bias[None, :]).astype(jnp.bfloat16)
    shard_sums = lax.psum(jnp.sum(own_rows.astype(jnp.float32), axis=1), "tp")
    checksum = lax.all_gather(shard_sums, ("role", "dp"), axis=0, tiled=True)
    return (incoming, probe_keys, checksum)


def solution(mesh):
    placed = (P("tp", ("role", "dp")), P("tp"), P(("role", "dp"), None))
    return jax.shard_map(
        body,
        mesh=mesh,
        in_specs=placed,
        out_specs=(P(None, "tp"), P(("role", "dp"), "tp"), P()),
        check_vma=False,
    )
```

profile of v0, /device:TPU:1, one launch (start us, length us, event | category | flops | bytes accessed | tf_op | source)
XLA Modules:
  0.0 74.8 jit_solution(112167562255301421)
XLA Ops:
  7.2 0.0 all-gather.2.cloned.1.call-start
  7.2 2.2 %copy.7 = bf16[256,1024]{0,1:T(8,128)(2,1)} copy(f32[256,1024]{1,0:T(8,128)} %param.3) | data formatting | bytes 1572864 | tf_op args[0]
  9.4 0.0 all-gather.2.cloned.1.call-update
  9.5 1.3 %convert_reduce_fusion = f32[1024]{0:T(1024)S(1)} fusion(bf16[256,1024]{0,1:T(8,128)(2,1)} %copy.7), kind=kLoop, calls=%fused_computation.2 | loop fusion | flops 523264 | bytes 528384 | tf_op jit(solution)/shard_map/reduce_sum | solution.py:12
  10.7 8.7 %psum.7 = f32[1024]{0:T(1024)S(1)} all-reduce(f32[1024]{0:T(1024)S(1)} %convert_reduce_fusion), channel_id=1, replica_groups=mesh['role'=4,'tp'=4,'dp'=2] {'tp'}, use_global_device_ids=true, to_apply=%region_1.0 | all-reduce | flops 1024 | bytes 8192 | tf_op jit(solution)/shard_map/psum | solution.py:12
  19.4 17.3 %all_gather.7 = f32[8192]{0:T(1024)S(1)} all-gather(f32[1024]{0:T(1024)S(1)} %psum.7), channel_id=1, replica_groups=mesh['role'=4,'tp'=4,'dp'=2] {'role','dp'}, dimensions={0}, use_global_device_ids=true | all-gather | bytes 36864 | tf_op jit(solution)/shard_map/all_gather | solution.py:13
  36.8 23.0 %all-gather.2.cloned.1.call-done = bf16[8192,256]{1,0:T(8,128)(2,1)} async-done(((bf16[1024,256]{1,0:T(8,128)(2,1)}), bf16[8192,256]{1,0:T(8,128)(2,1)}) %all-gather.2.cloned.1.call-update) | async-done | bytes 4194320 | tf_op jit(solution)/shard_map/all_gather | solution.py:9
  59.8 0.0 copy-start
  59.8 5.5 %fusion = bf16[256,256]{1,0:T(8,128)(2,1)} fusion(bf16[256,8192]{1,0:T(8,128)(2,1)} %param.5, bf16[8192,256]{1,0:T(8,128)(2,1)} %all-gather.2.cloned.1.call-done, f32[256]{0:T(256)} %param.4), kind=kOutput, calls=%fused_computation.1 | convolution fusion | flops 1073872896 | bytes 8520704 | tf_op jit(solution)/shard_map/dot_general | solution.py:10
  65.3 0.0 copy-done
  65.3 2.0 %copy.10 = bf16[8192,256]{1,0:T(8,128)(2,1)} copy(bf16[8192,256]{1,0:T(8,128)(2,1)S(1)} %copy-done) | data formatting | bytes 8388608
  67.3 0.6 copy.11
Async XLA Ops:
  7.2 52.6 %all-gather.2.cloned.1.call-start = ((), (), s32[]{:S(2)}) async-start(), calls=%async_computation | async-start | bytes 4718592 | tf_op jit(solution)/shard_map/all_gather | solution.py:9
  59.8 5.5 %copy-start = (bf16[8192,256]{1,0:T(8,128)(2,1)S(1)}, bf16[8192,256]{1,0:T(8,128)(2,1)}, u32[]{:S(2)}) copy-start(bf16[8192,256]{1,0:T(8,128)(2,1)} %all-gather.2.cloned.1.call-done) | copy-start | bytes 12582916
Sparse Core Ops, SparseCore 0:
  10.1 49.5 all-gather.1
where the time goes:
time: 75.3 us; the launch traced here: 74.8 us
  blocking collectives  26.1 us (35%)
  waiting for transfers between devices  23 us (31%)
  between operations  14 us (19%)
  matrix products  5.51 us (7%)
  local copies, waits for them, and re-layouts  4.86 us (6%)
  other arithmetic  1.25 us (2%)
    all_gather x1, waiting for transfers between devices, body(): incoming = lax.all_gather(own_rows, ('role', 'dp'), axis=0, tiled=True)  23 us
    all_gather x1, blocking collectives, body(): checksum = lax.all_gather(shard_sums, ('role', 'dp'), axis=0, tiled=True)  17.3 us
    psum x1, blocking collectives, body(): shard_sums = lax.psum(jnp.sum(own_rows.astype(jnp.float32), axis=1), 'tp')  8.72 us
    dot_general x1, matrix products, body(): totals = jnp.dot(probe_tokens, incoming, preferred_element_type=jnp.float32)  5.51 us
    unnamed x5, local copies, waits for them, and re-layouts  4.86 us
  transfers between devices with their start and end apart: 1, of which 1 were waited for; matrix products, arithmetic and copies ran while one was open for 2% of the time, Pallas kernels for 0%

commit v1 on v0

v1 whole, which is shorter than its diff:
```python
import functools

import jax
import jax.numpy as jnp
from jax import lax
from jax.experimental import pallas as pl
from jax.experimental.pallas import tpu as pltpu
from jax.sharding import PartitionSpec as P

MESH = pl.DeviceIdType.MESH


def gather_kernel(
    n, reps, heads, rows, chunk,
    master, bias, probe, full, keys, sums,
    slab, tokens, acc, part, got,
    slab_sem, token_sem, send_sem, line_sem, pass_sem, peer_sem,
    part_send, part_recv, sum_send, sum_recv, sum_pass, sum_peer,
):
    pieces = rows // chunk
    me, rep, head = lax.axis_index("role"), lax.axis_index("dp"), lax.axis_index("tp")
    has_left, has_right = me > 0, me < n - 1
    bits = [1 << s for s in range(heads.bit_length() - 1)]

    def pair(bit):
        return head + bit * (1 - 2 * lax.rem(lax.div(head, bit), 2))

    def peer_of(p):
        return lax.rem(rep + 1 + p, reps)

    barrier = pltpu.get_barrier_semaphore()

    @pl.when(has_left)
    def _():
        pl.semaphore_signal(barrier, inc=1, device_id={"role": me - 1}, device_id_type=MESH)

    @pl.when(has_right)
    def _():
        pl.semaphore_signal(barrier, inc=1, device_id={"role": me + 1}, device_id_type=MESH)

    @pl.loop(0, reps - 1)
    def _(p):
        pl.semaphore_signal(barrier, inc=1, device_id={"dp": peer_of(p)}, device_id_type=MESH)

    for bit in bits:
        pl.semaphore_signal(barrier, inc=1, device_id={"tp": pair(bit)}, device_id_type=MESH)

    def slab_copy(k):
        return pltpu.make_async_copy(
            master.at[:, pl.ds(k * chunk, chunk)], slab.at[k], slab_sem.at[k]
        )

    token_copy = pltpu.make_async_copy(probe, tokens, token_sem)
    for k in range(pieces):
        slab_copy(k).start()
    token_copy.start()

    def at(r, d, k):
        start = (r * reps + d) * rows + k * chunk
        return full.at[pl.ds(pl.multiple_of(start, chunk), chunk)]

    def line(r, k, way):
        return pltpu.make_async_remote_copy(
            src_ref=at(r, rep, k), dst_ref=at(r, rep, k),
            send_sem=send_sem.at[way, r, k], recv_sem=line_sem.at[r, k],
            device_id={"role": me + 2 * way - 1}, device_id_type=MESH,
        )

    def share(r, k, p):
        return pltpu.make_async_remote_copy(
            src_ref=at(r, rep, k), dst_ref=at(r, rep, k),
            send_sem=pass_sem.at[p, r, k], recv_sem=peer_sem.at[rep, r, k],
            device_id={"dp": peer_of(p)}, device_id_type=MESH,
        )

    def wait_line(r, k):
        pltpu.make_async_copy(at(r, rep, k), at(r, rep, k), line_sem.at[r, k]).wait()

    def wait_peer(r, d, k):
        pltpu.make_async_copy(at(r, d, k), at(r, d, k), peer_sem.at[d, r, k]).wait()

    def sum_line(r, way):
        b = r * reps + rep
        return pltpu.make_async_remote_copy(
            src_ref=sums.at[b], dst_ref=sums.at[b],
            send_sem=sum_send.at[way, r], recv_sem=sum_recv.at[r],
            device_id={"role": me + 2 * way - 1}, device_id_type=MESH,
        )

    def sum_share(r, p):
        b = r * reps + rep
        return pltpu.make_async_remote_copy(
            src_ref=sums.at[b], dst_ref=sums.at[b],
            send_sem=sum_pass.at[p, r], recv_sem=sum_peer.at[rep, r],
            device_id={"dp": peer_of(p)}, device_id_type=MESH,
        )

    def send_own(k):
        @pl.when(has_left)
        def _():
            line(me, k, 0).start()

        @pl.when(has_right)
        def _():
            line(me, k, 1).start()

        @pl.loop(0, reps - 1)
        def _(p):
            share(me, k, p).start()

    for k in range(pieces):
        slab_copy(k).wait()
        block = slab[k].astype(jnp.bfloat16).astype(jnp.float32)
        at(me, rep, k)[...] = jnp.transpose(block).astype(jnp.bfloat16)
        part[0, k : k + 1, :] = jnp.sum(block, axis=0, keepdims=True)
        if k == 0:
            beside = jnp.where(has_left & has_right, 2, 1) if n > 2 else n - 1
            pl.semaphore_wait(barrier, reps - 1 + len(bits) + beside)
        else:
            send_own(k - 1)
    acc[...] = jnp.broadcast_to(bias[...], acc.shape)
    send_own(pieces - 1)

    def trade(s):
        return pltpu.make_async_remote_copy(
            src_ref=part.at[s], dst_ref=got.at[s],
            send_sem=part_send.at[s], recv_sem=part_recv.at[s],
            device_id={"tp": pair(bits[s])}, device_id_type=MESH,
        )

    early = chunk % 128 == 0

    def add_dot(r, d, k):
        if early:
            start = (r * reps + d) * rows + k * chunk
            cols = pl.ds(pl.multiple_of(start, chunk), chunk)
            acc[...] += jnp.dot(
                tokens[:, cols], at(r, d, k)[...], preferred_element_type=jnp.float32
            )

    def peers_done(r, k):
        @pl.loop(0, reps - 1)
        def _(p):
            d = peer_of(p)
            wait_peer(r, d, k)
            add_dot(r, d, k)

    trade(0).start()
    token_copy.wait()

    @pl.loop(0, pieces)
    def _(k):
        add_dot(me, rep, k)

    for s in range(len(bits)):
        trade(s).wait_recv()
        total = part[s] + got[s]
        if s + 1 < len(bits):
            part[s + 1] = total
        else:
            sums[me * reps + rep] = total
        half = (pieces * s // len(bits), pieces * (s + 1) // len(bits))

        @pl.loop(half[0], half[1])
        def _(k):
            peers_done(me, k)

        if s + 1 < len(bits):
            trade(s + 1).start()

    @pl.when(has_left)
    def _():
        sum_line(me, 0).start()

    @pl.when(has_right)
    def _():
        sum_line(me, 1).start()

    @pl.loop(0, reps - 1)
    def _(p):
        sum_share(me, p).start()

    def sides(h):
        low, high = me - h, me + h
        return (
            (low, low >= 0, has_right, 1),
            (high, high < n, has_left, 0),
        )

    def step(t, fresh, lagged):
        if fresh:
            h, k = 1 + lax.div(t, pieces), lax.rem(t, pieces)
            for r, here, onward, way in sides(h):
                @pl.when(here)
                def _():
                    wait_line(r, k)

                    @pl.when(onward)
                    def _():
                        line(r, k, way).start()

                    @pl.loop(0, reps - 1)
                    def _(p):
                        share(r, k, p).start()

                    @pl.when(k == pieces - 1)
                    def _():
                        b = r * reps + rep
                        pltpu.make_async_copy(sums.at[b], sums.at[b], sum_recv.at[r]).wait()

                        @pl.when(onward)
                        def _():
                            sum_line(r, way).start()

                        @pl.loop(0, reps - 1)
                        def _(p):
                            sum_share(r, p).start()

            for r, here, onward, way in sides(h):
                @pl.when(here)
                def _():
                    add_dot(r, rep, k)

        if lagged:
            h, k = 1 + lax.div(t - 1, pieces), lax.rem(t - 1, pieces)
            for r, here, onward, way in sides(h):
                @pl.when(here)
                def _():
                    peers_done(r, k)

    steps = (n - 1) * pieces
    step(jnp.int32(0), True, False)

    @pl.loop(1, steps)
    def _(t):
        step(t, True, True)

    step(jnp.int32(steps), False, True)

    @pl.loop(0, n)
    def _(r):
        @pl.loop(0, reps - 1)
        def _(p):
            b = r * reps + peer_of(p)
            pltpu.make_async_copy(sums.at[b], sums.at[b], sum_peer.at[peer_of(p), r]).wait()
            sum_share(r, p).wait_send()

        for onward, way in (((r >= me) & has_left, 0), ((r <= me) & has_right, 1)):
            @pl.when(onward)
            def _():
                sum_line(r, way).wait_send()

        @pl.loop(0, pieces)
        def _(k):
            @pl.loop(0, reps - 1)
            def _(p):
                share(r, k, p).wait_send()

            for onward, way in (((r >= me) & has_left, 0), ((r <= me) & has_right, 1)):
                @pl.when(onward)
                def _():
                    line(r, k, way).wait_send()

    for s in range(len(bits)):
        trade(s).wait_send()

    if not early:
        tile = 512

        @pl.loop(0, tokens.shape[1] // tile)
        def _(i):
            span = pl.ds(pl.multiple_of(i * tile, tile), tile)
            acc[...] += jnp.dot(
                tokens[:, span], full[span, :], preferred_element_type=jnp.float32
            )

    keys[...] = acc[...].astype(keys.dtype)


def store_kernel(full, keys, sums, weight, probe_keys, checksum, sems):
    parts = 8
    size = full.shape[0] // parts
    copies = [
        pltpu.make_async_copy(
            full.at[pl.ds(i * size, size)], weight.at[pl.ds(i * size, size)], sems.at[i]
        )
        for i in range(parts)
    ]
    copies.append(pltpu.make_async_copy(keys, probe_keys, sems.at[parts]))
    copies.append(pltpu.make_async_copy(sums, checksum, sems.at[parts + 1]))
    for copy in copies:
        copy.start()
    for copy in copies:
        copy.wait()


def body(mesh, master, key_bias, probe_tokens):
    n, reps, heads = mesh.shape["role"], mesh.shape["dp"], mesh.shape["tp"]
    feats, rows = master.shape
    probes, width = probe_tokens.shape
    chunk = min(128, rows)
    pieces, blocks = rows // chunk, n * reps
    levels = heads.bit_length() - 1
    vmem, hbm = pl.BlockSpec(memory_space=pltpu.VMEM), pl.BlockSpec(memory_space=pl.ANY)
    dma = pltpu.SemaphoreType.DMA
    others = max(reps - 1, 1)
    full, keys, sums = pl.pallas_call(
        functools.partial(gather_kernel, n, reps, heads, rows, chunk),
        out_shape=(
            pltpu.VMEM((width, feats), jnp.bfloat16),
            pltpu.VMEM((probes, feats), jnp.bfloat16),
            pltpu.VMEM((blocks, pieces, chunk), jnp.float32),
        ),
        in_specs=[hbm, vmem, hbm],
        out_specs=(vmem, vmem, vmem),
        scratch_shapes=[
            pltpu.VMEM((pieces, feats, chunk), jnp.float32),
            pltpu.VMEM((probes, width), jnp.bfloat16),
            pltpu.VMEM((probes, feats), jnp.float32),
            pltpu.VMEM((levels, pieces, chunk), jnp.float32),
            pltpu.VMEM((levels, pieces, chunk), jnp.float32),
            dma((pieces,)),
            dma,
            dma((2, n, pieces)),
            dma((n, pieces)),
            dma((others, n, pieces)),
            dma((reps, n, pieces)),
            dma((levels,)),
            dma((levels,)),
            dma((2, n)),
            dma((n,)),
            dma((others, n)),
            dma((reps, n)),
        ],
        compiler_params=pltpu.CompilerParams(
            collective_id=0, has_side_effects=True, vmem_limit_bytes=24 * 2**20
        ),
        name="gather",
    )(
        pltpu.with_memory_space_constraint(master, pltpu.HBM),
        key_bias.reshape(1, feats),
        pltpu.with_memory_space_constraint(probe_tokens, pltpu.HBM),
    )
    weight, probe_keys, checksum = pl.pallas_call(
        store_kernel,
        out_shape=(
            jax.ShapeDtypeStruct(full.shape, full.dtype),
            jax.ShapeDtypeStruct(keys.shape, keys.dtype),
            jax.ShapeDtypeStruct(sums.shape, sums.dtype),
        ),
        in_specs=[vmem] * 3,
        out_specs=(hbm,) * 3,
        scratch_shapes=[dma((10,))],
        compiler_params=pltpu.CompilerParams(vmem_limit_bytes=2**20),
        name="store",
    )(*(pltpu.with_memory_space_constraint(x, pltpu.VMEM) for x in (full, keys, sums)))
    return weight, probe_keys, checksum.reshape(-1)


def solution(mesh):
    placed = (P("tp", ("role", "dp")), P("tp"), P(("role", "dp"), None))
    return jax.shard_map(
        functools.partial(body, mesh),
        mesh=mesh,
        in_specs=placed,
        out_specs=(P(None, "tp"), P(("role", "dp"), "tp"), P()),
        check_vma=False,
    )
```

time: 75.3 us -> 46 us (0.61)
  Pallas kernels: 0 us -> 44.5 us
  blocking collectives: 26.1 us -> 0 us
  waiting for transfers between devices: 23 us -> 0 us
  between operations: 14 us -> 0.65 us
  matrix products: 5.51 us -> 0 us
  local copies, waits for them, and re-layouts: 4.86 us -> 0.67 us
  other arithmetic: 1.25 us -> 0 us
    pallas_call x0 -> x2, Pallas kernels: none -> 44.5 us  [the longest x1 42.4 us: body(): pl.pallas_call(functools.partial(gather_kernel, n, reps, heads, rows, chu...]
    all_gather x1 -> x0, waiting for transfers between devices: 23 us -> none  [body(): incoming = lax.all_gather(own_rows, ('role', 'dp'), axis=0, tiled=True)]
    all_gather x1 -> x0, blocking collectives: 17.3 us -> none  [body(): checksum = lax.all_gather(shard_sums, ('role', 'dp'), axis=0, tiled=True)]
    psum x1 -> x0, blocking collectives: 8.72 us -> none  [body(): shard_sums = lax.psum(jnp.sum(own_rows.astype(jnp.float32), axis=1), 'tp')]
    dot_general x1 -> x0, matrix products: 5.51 us -> none  [body(): totals = jnp.dot(probe_tokens, incoming, preferred_element_type=jnp.float32)]
    unnamed x5 -> x2, local copies, waits for them, and re-layouts: 4.86 us -> 0.67 us
    reduce_sum x1 -> x0, other arithmetic: 1.25 us -> none  [body(): shard_sums = lax.psum(jnp.sum(own_rows.astype(jnp.float32), axis=1), 'tp')]
  transfers between devices with their start and end apart: 1 -> 0, of which waited for: 1 -> 0; matrix products, arithmetic and copies ran while one was open for 2% -> 0% of each run, Pallas kernels for 0% -> 0%
where the time goes in v1:
time: 46 us; the launch traced here: 45.9 us
  Pallas kernels  44.5 us (97%)
  local copies, waits for them, and re-layouts  0.67 us (1%)
  between operations  0.65 us (1%)
    pallas_call x1, Pallas kernels, body(): pl.pallas_call(functools.partial(gather_kernel, n, reps, heads, rows, chu...  42.4 us
    pallas_call x1, Pallas kernels, body(): pl.pallas_call(store_kernel, out_shape=(jax.ShapeDtypeStruct(full.shape,...  2.13 us

profile of v1, /device:TPU:1, one launch (start us, length us, event | category | flops | bytes accessed | tf_op | source)
XLA Modules:
  0.0 45.9 jit_solution(4170881697994017677)
XLA Ops:
  0.6 0.0 copy-start
  0.6 0.7 %copy-done = f32[256]{0:T(256)S(1)} copy-done((f32[256]{0:T(256)S(1)}, f32[256]{0:T(256)}, u32[]{:S(2)}) %copy-start) | copy-done | bytes 1048
  1.3 42.4 %gather.1 = (bf16[8192,256]{1,0:T(8,128)(2,1)S(1)}, bf16[256,256]{1,0:T(8,128)(2,1)S(1)}, f32[8,8,128]{2,1,0:T(8,128)S(1)}) custom-call(f32[256,1024]{1,0:T(8,128)} %master.1, f32[1,256]{1,0:T(1,128)S(1)} %bitcast.2, bf16[256,8192]{1,0:T(8,128)(2,1)} %probe.1), custom_call_target="tpu_custom_call" | custom-call | tf_op jit(solution)/shard_map/gather/pallas_call | solution.py:307
  43.7 2.1 %store.1 = (bf16[8192,256]{1,0:T(8,128)(2,1)}, bf16[256,256]{1,0:T(8,128)(2,1)}, f32[8,8,128]{2,1,0:T(8,128)}) custom-call(bf16[8192,256]{1,0:T(8,128)(2,1)S(1)} %get-tuple-element.9.full, bf16[256,256]{1,0:T(8,128)(2,1)S(1)} %get-tuple-element.10.keys, f32[8,8,128]{2,1,0:T(8,128)S(1)} %get-tuple-element.11.sums), custom_call_target="tpu_custom_call" | custom-call | tf_op jit(solution)/shard_map/store/pallas_call | solution.py:344
Async XLA Ops:
  0.6 0.7 %copy-start = (f32[256]{0:T(256)S(1)}, f32[256]{0:T(256)}, u32[]{:S(2)}) copy-start(f32[256]{0:T(256)} %param.4) | copy-start | bytes 3076

commit v2 on v1

--- a/solution.py
+++ b/solution.py
@@ -13,8 +13,8 @@
 def gather_kernel(
     n, reps, heads, rows, chunk,
     master, bias, probe, full, keys, sums,
-    slab, tokens, acc, part, got,
-    slab_sem, token_sem, send_sem, line_sem, pass_sem, peer_sem,
+    slab, tokens, offset, acc, part, got,
+    slab_sem, token_sem, bias_sem, send_sem, line_sem, pass_sem, peer_sem,
     part_send, part_recv, sum_send, sum_recv, sum_pass, sum_peer,
 ):
     pieces = rows // chunk
@@ -45,15 +45,23 @@
     for bit in bits:
         pl.semaphore_signal(barrier, inc=1, device_id={"tp": pair(bit)}, device_id_type=MESH)
 
-    def slab_copy(k):
-        return pltpu.make_async_copy(
-            master.at[:, pl.ds(k * chunk, chunk)], slab.at[k], slab_sem.at[k]
-        )
-
+    def slab_copy(i):
+        cols = pl.ds(0, chunk) if i == 0 else pl.ds(chunk, rows - chunk)
+        return pltpu.make_async_copy(master.at[:, cols], slab.at[:, cols], slab_sem.at[i])
+
+    slabs = min(pieces, 2)
     token_copy = pltpu.make_async_copy(probe, tokens, token_sem)
-    for k in range(pieces):
-        slab_copy(k).start()
+    bias_copy = pltpu.make_async_copy(bias, offset, bias_sem)
+    for i in range(slabs):
+        slab_copy(i).start()
+    bias_copy.start()
     token_copy.start()
+
+    def block(r, d):
+        return full.at[pl.ds(pl.multiple_of((r * reps + d) * rows, chunk), rows)]
+
+    def slot(r, owner):
+        return lax.rem(r - owner + 2 * n - 1, n)
 
     def at(r, d, k):
         start = (r * reps + d) * rows + k * chunk
@@ -62,28 +70,31 @@
     def line(r, k, way):
         return pltpu.make_async_remote_copy(
             src_ref=at(r, rep, k), dst_ref=at(r, rep, k),
-            send_sem=send_sem.at[way, r, k], recv_sem=line_sem.at[r, k],
+            send_sem=send_sem.at[way, r],
+            recv_sem=line_sem.at[slot(r, me + 2 * way - 1), k],
             device_id={"role": me + 2 * way - 1}, device_id_type=MESH,
         )
 
     def share(r, k, p):
         return pltpu.make_async_remote_copy(
             src_ref=at(r, rep, k), dst_ref=at(r, rep, k),
-            send_sem=pass_sem.at[p, r, k], recv_sem=peer_sem.at[rep, r, k],
+            send_sem=pass_sem.at[p, r], recv_sem=peer_sem.at[reps - 2 - p, r, k],
             device_id={"dp": peer_of(p)}, device_id_type=MESH,
         )
 
     def wait_line(r, k):
-        pltpu.make_async_copy(at(r, rep, k), at(r, rep, k), line_sem.at[r, k]).wait()
-
-    def wait_peer(r, d, k):
-        pltpu.make_async_copy(at(r, d, k), at(r, d, k), peer_sem.at[d, r, k]).wait()
+        pltpu.make_async_copy(at(r, rep, k), at(r, rep, k), line_sem.at[slot(r, me), k]).wait()
+
+    def wait_peer(r, p, k):
+        here = at(r, peer_of(p), k)
+        pltpu.make_async_copy(here, here, peer_sem.at[p, r, k]).wait()
 
     def sum_line(r, way):
         b = r * reps + rep
         return pltpu.make_async_remote_copy(
             src_ref=sums.at[b], dst_ref=sums.at[b],
-            send_sem=sum_send.at[way, r], recv_sem=sum_recv.at[r],
+            send_sem=sum_send.at[way, r],
+            recv_sem=sum_recv.at[slot(r, me + 2 * way - 1)],
             device_id={"role": me + 2 * way - 1}, device_id_type=MESH,
         )
 
@@ -91,7 +102,7 @@
         b = r * reps + rep
         return pltpu.make_async_remote_copy(
             src_ref=sums.at[b], dst_ref=sums.at[b],
-            send_sem=sum_pass.at[p, r], recv_sem=sum_peer.at[rep, r],
+            send_sem=sum_pass.at[p, r], recv_sem=sum_peer.at[reps - 2 - p, r],
             device_id={"dp": peer_of(p)}, device_id_type=MESH,
         )
 
@@ -109,16 +120,18 @@
             share(me, k, p).start()
 
     for k in range(pieces):
-        slab_copy(k).wait()
-        block = slab[k].astype(jnp.bfloat16).astype(jnp.float32)
-        at(me, rep, k)[...] = jnp.transpose(block).astype(jnp.bfloat16)
-        part[0, k : k + 1, :] = jnp.sum(block, axis=0, keepdims=True)
-        if k == 0:
+        if k < 2:
+            slab_copy(k).wait()
+        held = slab[:, k * chunk : (k + 1) * chunk].astype(jnp.bfloat16).astype(jnp.float32)
+        at(me, rep, k)[...] = jnp.transpose(held).astype(jnp.bfloat16)
+        part[0, k : k + 1, :] = jnp.sum(held, axis=0, keepdims=True)
+        if k == min(1, pieces - 1):
             beside = jnp.where(has_left & has_right, 2, 1) if n > 2 else n - 1
             pl.semaphore_wait(barrier, reps - 1 + len(bits) + beside)
-        else:
+        if k:
             send_own(k - 1)
-    acc[...] = jnp.broadcast_to(bias[...], acc.shape)
+    bias_copy.wait()
+    acc[...] = jnp.broadcast_to(offset[...], acc.shape)
     send_own(pieces - 1)
 
     def trade(s):
@@ -141,9 +154,8 @@
     def peers_done(r, k):
         @pl.loop(0, reps - 1)
         def _(p):
-            d = peer_of(p)
-            wait_peer(r, d, k)
-            add_dot(r, d, k)
+            wait_peer(r, p, k)
+            add_dot(r, peer_of(p), k)
 
     trade(0).start()
     token_copy.wait()
@@ -206,7 +218,7 @@
                     @pl.when(k == pieces - 1)
                     def _():
                         b = r * reps + rep
-                        pltpu.make_async_copy(sums.at[b], sums.at[b], sum_recv.at[r]).wait()
+                        pltpu.make_async_copy(sums.at[b], sums.at[b], sum_recv.at[slot(r, me)]).wait()
 
                         @pl.when(onward)
                         def _():
@@ -239,27 +251,20 @@
 
     @pl.loop(0, n)
     def _(r):
+        own = block(r, rep)
+
         @pl.loop(0, reps - 1)
         def _(p):
             b = r * reps + peer_of(p)
-            pltpu.make_async_copy(sums.at[b], sums.at[b], sum_peer.at[peer_of(p), r]).wait()
+            pltpu.make_async_copy(sums.at[b], sums.at[b], sum_peer.at[p, r]).wait()
             sum_share(r, p).wait_send()
+            pltpu.make_async_copy(own, own, pass_sem.at[p, r]).wait()
 
         for onward, way in (((r >= me) & has_left, 0), ((r <= me) & has_right, 1)):
             @pl.when(onward)
             def _():
                 sum_line(r, way).wait_send()
-
-        @pl.loop(0, pieces)
-        def _(k):
-            @pl.loop(0, reps - 1)
-            def _(p):
-                share(r, k, p).wait_send()
-
-            for onward, way in (((r >= me) & has_left, 0), ((r <= me) & has_right, 1)):
-                @pl.when(onward)
-                def _():
-                    line(r, k, way).wait_send()
+                pltpu.make_async_copy(own, own, send_sem.at[way, r]).wait()
 
     for s in range(len(bits)):
         trade(s).wait_send()
@@ -311,26 +316,28 @@
             pltpu.VMEM((probes, feats), jnp.bfloat16),
             pltpu.VMEM((blocks, pieces, chunk), jnp.float32),
         ),
-        in_specs=[hbm, vmem, hbm],
+        in_specs=[hbm, hbm, hbm],
         out_specs=(vmem, vmem, vmem),
         scratch_shapes=[
-            pltpu.VMEM((pieces, feats, chunk), jnp.float32),
+            pltpu.VMEM((feats, rows), jnp.float32),
             pltpu.VMEM((probes, width), jnp.bfloat16),
+            pltpu.VMEM((1, feats), jnp.float32),
             pltpu.VMEM((probes, feats), jnp.float32),
             pltpu.VMEM((levels, pieces, chunk), jnp.float32),
             pltpu.VMEM((levels, pieces, chunk), jnp.float32),
-            dma((pieces,)),
+            dma((min(pieces, 2),)),
             dma,
-            dma((2, n, pieces)),
-            dma((n, pieces)),
+            dma,
+            dma((2, n)),
+            dma((n - 1, pieces)),
+            dma((others, n)),
             dma((others, n, pieces)),
-            dma((reps, n, pieces)),
             dma((levels,)),
             dma((levels,)),
             dma((2, n)),
-            dma((n,)),
+            dma((n - 1,)),
             dma((others, n)),
-            dma((reps, n)),
+            dma((others, n)),
         ],
         compiler_params=pltpu.CompilerParams(
             collective_id=0, has_side_effects=True, vmem_limit_bytes=24 * 2**20
@@ -338,7 +345,7 @@
         name="gather",
     )(
         pltpu.with_memory_space_constraint(master, pltpu.HBM),
-        key_bias.reshape(1, feats),
+        pltpu.with_memory_space_constraint(key_bias.reshape(1, feats), pltpu.HBM),
         pltpu.with_memory_space_constraint(probe_tokens, pltpu.HBM),
     )
     weight, probe_keys, checksum = pl.pallas_call(

time: 46 us -> 43.8 us (0.952)
  Pallas kernels: 44.5 us -> 43.1 us
  local copies, waits for them, and re-layouts: 0.67 us -> 0 us
    pallas_call x1, Pallas kernels: 42.4 us -> 40.9 us  [body(): pl.pallas_call(functools.partial(gather_kernel, n, reps, heads, rows, chu...]
    unnamed x2 -> x0, local copies, waits for them, and re-layouts: 0.67 us -> none
where the time goes in v2:
time: 43.8 us; the launch traced here: 43.7 us
  Pallas kernels  43.1 us (98%)
  between operations  0.64 us (1%)
    pallas_call x1, Pallas kernels, body(): pl.pallas_call(functools.partial(gather_kernel, n, reps, heads, rows, chu...  40.9 us
    pallas_call x1, Pallas kernels, body(): pl.pallas_call(store_kernel, out_shape=(jax.ShapeDtypeStruct(full.shape,...  2.13 us

profile of v2, /device:TPU:1, one launch (start us, length us, event | category | flops | bytes accessed | tf_op | source)
XLA Modules:
  0.0 43.7 jit_solution(12012139472152858058)
XLA Ops:
  0.6 40.9 %gather.1 = (bf16[8192,256]{1,0:T(8,128)(2,1)S(1)}, bf16[256,256]{1,0:T(8,128)(2,1)S(1)}, f32[8,8,128]{2,1,0:T(8,128)S(1)}) custom-call(f32[256,1024]{1,0:T(8,128)} %master.1, f32[1,256]{1,0:T(1,128)} %bitcast.2, bf16[256,8192]{1,0:T(8,128)(2,1)} %probe.1), custom_call_target="tpu_custom_call" | custom-call | tf_op jit(solution)/shard_map/gather/pallas_call | solution.py:312
  41.6 2.1 %store.1 = (bf16[8192,256]{1,0:T(8,128)(2,1)}, bf16[256,256]{1,0:T(8,128)(2,1)}, f32[8,8,128]{2,1,0:T(8,128)}) custom-call(bf16[8192,256]{1,0:T(8,128)(2,1)S(1)} %get-tuple-element.9.full, bf16[256,256]{1,0:T(8,128)(2,1)S(1)} %get-tuple-element.10.keys, f32[8,8,128]{2,1,0:T(8,128)S(1)} %get-tuple-element.11.sums), custom_call_target="tpu_custom_call" | custom-call | tf_op jit(solution)/shard_map/store/pallas_call | solution.py:351

commit v3 on v2

--- a/solution.py
+++ b/solution.py
@@ -18,11 +18,13 @@
     part_send, part_recv, sum_send, sum_recv, sum_pass, sum_peer,
 ):
     pieces = rows // chunk
+    pair = 2 if pieces % 2 == 0 else 1
+    span = pair * chunk
     me, rep, head = lax.axis_index("role"), lax.axis_index("dp"), lax.axis_index("tp")
     has_left, has_right = me > 0, me < n - 1
     bits = [1 << s for s in range(heads.bit_length() - 1)]
 
-    def pair(bit):
+    def partner(bit):
         return head + bit * (1 - 2 * lax.rem(lax.div(head, bit), 2))
 
     def peer_of(p):
@@ -43,13 +45,15 @@
         pl.semaphore_signal(barrier, inc=1, device_id={"dp": peer_of(p)}, device_id_type=MESH)
 
     for bit in bits:
-        pl.semaphore_signal(barrier, inc=1, device_id={"tp": pair(bit)}, device_id_type=MESH)
+        pl.semaphore_signal(barrier, inc=1, device_id={"tp": partner(bit)}, device_id_type=MESH)
+
+    cuts = sorted({0, chunk, min(2, pieces) * chunk, rows})
 
     def slab_copy(i):
-        cols = pl.ds(0, chunk) if i == 0 else pl.ds(chunk, rows - chunk)
+        cols = pl.ds(cuts[i], cuts[i + 1] - cuts[i])
         return pltpu.make_async_copy(master.at[:, cols], slab.at[:, cols], slab_sem.at[i])
 
-    slabs = min(pieces, 2)
+    slabs = len(cuts) - 1
     token_copy = pltpu.make_async_copy(probe, tokens, token_sem)
     bias_copy = pltpu.make_async_copy(bias, offset, bias_sem)
     for i in range(slabs):
@@ -57,9 +61,6 @@
     bias_copy.start()
     token_copy.start()
 
-    def block(r, d):
-        return full.at[pl.ds(pl.multiple_of((r * reps + d) * rows, chunk), rows)]
-
     def slot(r, owner):
         return lax.rem(r - owner + 2 * n - 1, n)
 
@@ -67,33 +68,37 @@
         start = (r * reps + d) * rows + k * chunk
         return full.at[pl.ds(pl.multiple_of(start, chunk), chunk)]
 
+    def group(r, d, g):
+        start = (r * reps + d) * rows + g * span
+        return full.at[pl.ds(pl.multiple_of(start, span), span)]
+
     def line(r, k, way):
         return pltpu.make_async_remote_copy(
             src_ref=at(r, rep, k), dst_ref=at(r, rep, k),
-            send_sem=send_sem.at[way, r],
+            send_sem=send_sem.at[way],
             recv_sem=line_sem.at[slot(r, me + 2 * way - 1), k],
             device_id={"role": me + 2 * way - 1}, device_id_type=MESH,
         )
 
-    def share(r, k, p):
-        return pltpu.make_async_remote_copy(
-            src_ref=at(r, rep, k), dst_ref=at(r, rep, k),
-            send_sem=pass_sem.at[p, r], recv_sem=peer_sem.at[reps - 2 - p, r, k],
+    def share(r, g, p):
+        return pltpu.make_async_remote_copy(
+            src_ref=group(r, rep, g), dst_ref=group(r, rep, g),
+            send_sem=pass_sem.at[p], recv_sem=peer_sem.at[reps - 2 - p, r, g],
             device_id={"dp": peer_of(p)}, device_id_type=MESH,
         )
 
     def wait_line(r, k):
         pltpu.make_async_copy(at(r, rep, k), at(r, rep, k), line_sem.at[slot(r, me), k]).wait()
 
-    def wait_peer(r, p, k):
-        here = at(r, peer_of(p), k)
-        pltpu.make_async_copy(here, here, peer_sem.at[p, r, k]).wait()
+    def wait_peer(r, p, g):
+        here = group(r, peer_of(p), g)
+        pltpu.make_async_copy(here, here, peer_sem.at[p, r, g]).wait()
 
     def sum_line(r, way):
         b = r * reps + rep
         return pltpu.make_async_remote_copy(
             src_ref=sums.at[b], dst_ref=sums.at[b],
-            send_sem=sum_send.at[way, r],
+            send_sem=sum_send.at[way],
             recv_sem=sum_recv.at[slot(r, me + 2 * way - 1)],
             device_id={"role": me + 2 * way - 1}, device_id_type=MESH,
         )
@@ -102,7 +107,7 @@
         b = r * reps + rep
         return pltpu.make_async_remote_copy(
             src_ref=sums.at[b], dst_ref=sums.at[b],
-            send_sem=sum_pass.at[p, r], recv_sem=sum_peer.at[reps - 2 - p, r],
+            send_sem=sum_pass.at[p], recv_sem=sum_peer.at[reps - 2 - p],
             device_id={"dp": peer_of(p)}, device_id_type=MESH,
         )
 
@@ -115,12 +120,13 @@
         def _():
             line(me, k, 1).start()
 
-        @pl.loop(0, reps - 1)
-        def _(p):
-            share(me, k, p).start()
+        if k % pair == pair - 1:
+            @pl.loop(0, reps - 1)
+            def _(p):
+                share(me, k // pair, p).start()
 
     for k in range(pieces):
-        if k < 2:
+        if k < slabs:
             slab_copy(k).wait()
         held = slab[:, k * chunk : (k + 1) * chunk].astype(jnp.bfloat16).astype(jnp.float32)
         at(me, rep, k)[...] = jnp.transpose(held).astype(jnp.bfloat16)
@@ -138,31 +144,32 @@
         return pltpu.make_async_remote_copy(
             src_ref=part.at[s], dst_ref=got.at[s],
             send_sem=part_send.at[s], recv_sem=part_recv.at[s],
-            device_id={"tp": pair(bits[s])}, device_id_type=MESH,
+            device_id={"tp": partner(bits[s])}, device_id_type=MESH,
         )
 
     early = chunk % 128 == 0
 
-    def add_dot(r, d, k):
+    def add_dot(r, d, g):
         if early:
-            start = (r * reps + d) * rows + k * chunk
-            cols = pl.ds(pl.multiple_of(start, chunk), chunk)
+            start = (r * reps + d) * rows + g * span
+            cols = pl.ds(pl.multiple_of(start, span), span)
             acc[...] += jnp.dot(
-                tokens[:, cols], at(r, d, k)[...], preferred_element_type=jnp.float32
+                tokens[:, cols], group(r, d, g)[...], preferred_element_type=jnp.float32
             )
 
-    def peers_done(r, k):
+    def peers_done(r, g):
         @pl.loop(0, reps - 1)
         def _(p):
-            wait_peer(r, p, k)
-            add_dot(r, peer_of(p), k)
-
+            wait_peer(r, p, g)
+            add_dot(r, peer_of(p), g)
+
+    groups = pieces // pair
     trade(0).start()
     token_copy.wait()
 
-    @pl.loop(0, pieces)
-    def _(k):
-        add_dot(me, rep, k)
+    @pl.loop(0, groups)
+    def _(g):
+        add_dot(me, rep, g)
 
     for s in range(len(bits)):
         trade(s).wait_recv()
@@ -171,11 +178,10 @@
             part[s + 1] = total
         else:
             sums[me * reps + rep] = total
-        half = (pieces * s // len(bits), pieces * (s + 1) // len(bits))
-
-        @pl.loop(half[0], half[1])
-        def _(k):
-            peers_done(me, k)
+
+        @pl.loop(groups * s // len(bits), groups * (s + 1) // len(bits))
+        def _(g):
+            peers_done(me, g)
 
         if s + 1 < len(bits):
             trade(s + 1).start()
@@ -202,6 +208,7 @@
     def step(t, fresh, lagged):
         if fresh:
             h, k = 1 + lax.div(t, pieces), lax.rem(t, pieces)
+            g, whole = lax.div(k, pair), lax.rem(k, pair) == pair - 1
             for r, here, onward, way in sides(h):
                 @pl.when(here)
                 def _():
@@ -211,9 +218,11 @@
                     def _():
                         line(r, k, way).start()
 
-                    @pl.loop(0, reps - 1)
-                    def _(p):
-                        share(r, k, p).start()
+                    @pl.when(whole)
+                    def _():
+                        @pl.loop(0, reps - 1)
+                        def _(p):
+                            share(r, g, p).start()
 
                     @pl.when(k == pieces - 1)
                     def _():
@@ -229,16 +238,17 @@
                             sum_share(r, p).start()
 
             for r, here, onward, way in sides(h):
-                @pl.when(here)
+                @pl.when(here & whole)
                 def _():
-                    add_dot(r, rep, k)
+                    add_dot(r, rep, g)
 
         if lagged:
             h, k = 1 + lax.div(t - 1, pieces), lax.rem(t - 1, pieces)
+            g, whole = lax.div(k, pair), lax.rem(k, pair) == pair - 1
             for r, here, onward, way in sides(h):
-                @pl.when(here)
+                @pl.when(here & whole)
                 def _():
-                    peers_done(r, k)
+                    peers_done(r, g)
 
     steps = (n - 1) * pieces
     step(jnp.int32(0), True, False)
@@ -247,24 +257,24 @@
     def _(t):
         step(t, True, True)
 
+    def drain(ref, sem):
+        pltpu.make_async_copy(ref, ref, sem).wait()
+
+    for i in range(n):
+        @pl.when(me == i)
+        def _():
+            for way, count in ((0, n - i if i else 0), (1, i + 1 if i < n - 1 else 0)):
+                if count:
+                    drain(full.at[pl.ds(0, count * rows)], send_sem.at[way])
+                    drain(sums.at[pl.ds(0, count)], sum_send.at[way])
+
     step(jnp.int32(steps), False, True)
 
-    @pl.loop(0, n)
-    def _(r):
-        own = block(r, rep)
-
-        @pl.loop(0, reps - 1)
-        def _(p):
-            b = r * reps + peer_of(p)
-            pltpu.make_async_copy(sums.at[b], sums.at[b], sum_peer.at[p, r]).wait()
-            sum_share(r, p).wait_send()
-            pltpu.make_async_copy(own, own, pass_sem.at[p, r]).wait()
-
-        for onward, way in (((r >= me) & has_left, 0), ((r <= me) & has_right, 1)):
-            @pl.when(onward)
-            def _():
-                sum_line(r, way).wait_send()
-                pltpu.make_async_copy(own, own, send_sem.at[way, r]).wait()
+    @pl.loop(0, reps - 1)
+    def _(p):
+        drain(full.at[pl.ds(0, n * rows)], pass_sem.at[p])
+        drain(sums.at[pl.ds(0, n)], sum_pass.at[p])
+        drain(sums.at[pl.ds(0, n)], sum_peer.at[p])
 
     for s in range(len(bits)):
         trade(s).wait_send()
@@ -274,9 +284,9 @@
 
         @pl.loop(0, tokens.shape[1] // tile)
         def _(i):
-            span = pl.ds(pl.multiple_of(i * tile, tile), tile)
+            part_of = pl.ds(pl.multiple_of(i * tile, tile), tile)
             acc[...] += jnp.dot(
-                tokens[:, span], full[span, :], preferred_element_type=jnp.float32
+                tokens[:, part_of], full[part_of, :], preferred_element_type=jnp.float32
             )
 
     keys[...] = acc[...].astype(keys.dtype)
@@ -306,6 +316,7 @@
     chunk = min(128, rows)
     pieces, blocks = rows // chunk, n * reps
     levels = heads.bit_length() - 1
+    groups = pieces // 2 if pieces % 2 == 0 else pieces
     vmem, hbm = pl.BlockSpec(memory_space=pltpu.VMEM), pl.BlockSpec(memory_space=pl.ANY)
     dma = pltpu.SemaphoreType.DMA
     others = max(reps - 1, 1)
@@ -325,19 +336,19 @@
             pltpu.VMEM((probes, feats), jnp.float32),
             pltpu.VMEM((levels, pieces, chunk), jnp.float32),
             pltpu.VMEM((levels, pieces, chunk), jnp.float32),
-            dma((min(pieces, 2),)),
+            dma((min(pieces, 3),)),
             dma,
             dma,
-            dma((2, n)),
+            dma((2,)),
             dma((n - 1, pieces)),
-            dma((others, n)),
-            dma((others, n, pieces)),
+            dma((others,)),
+            dma((others, n, groups)),
             dma((levels,)),
             dma((levels,)),
-            dma((2, n)),
+            dma((2,)),
             dma((n - 1,)),
-            dma((others, n)),
-            dma((others, n)),
+            dma((others,)),
+            dma((others,)),
         ],
         compiler_params=pltpu.CompilerParams(
             collective_id=0, has_side_effects=True, vmem_limit_bytes=24 * 2**20

time: 43.8 us -> 43.5 us (level)
  no operation moved by 1% of the time
where the time goes in v3:
time: 43.5 us; the launch traced here: 43.3 us
  Pallas kernels  42.7 us (98%)
  between operations  0.64 us (1%)
    pallas_call x1, Pallas kernels, body(): pl.pallas_call(functools.partial(gather_kernel, n, reps, heads, rows, chu...  40.6 us
    pallas_call x1, Pallas kernels, body(): pl.pallas_call(store_kernel, out_shape=(jax.ShapeDtypeStruct(full.shape,...  2.13 us

profile of v3, /device:TPU:1, one launch (start us, length us, event | category | flops | bytes accessed | tf_op | source)
XLA Modules:
  0.0 43.3 jit_solution(306344237908024537)
XLA Ops:
  0.6 40.6 %gather.1 = (bf16[8192,256]{1,0:T(8,128)(2,1)S(1)}, bf16[256,256]{1,0:T(8,128)(2,1)S(1)}, f32[8,8,128]{2,1,0:T(8,128)S(1)}) custom-call(f32[256,1024]{1,0:T(8,128)} %master.1, f32[1,256]{1,0:T(1,128)} %bitcast.2, bf16[256,8192]{1,0:T(8,128)(2,1)} %probe.1), custom_call_target="tpu_custom_call" | custom-call | tf_op jit(solution)/shard_map/gather/pallas_call | solution.py:323
  41.2 2.1 %store.1 = (bf16[8192,256]{1,0:T(8,128)(2,1)}, bf16[256,256]{1,0:T(8,128)(2,1)}, f32[8,8,128]{2,1,0:T(8,128)}) custom-call(bf16[8192,256]{1,0:T(8,128)(2,1)S(1)} %get-tuple-element.9.full, bf16[256,256]{1,0:T(8,128)(2,1)S(1)} %get-tuple-element.10.keys, f32[8,8,128]{2,1,0:T(8,128)S(1)} %get-tuple-element.11.sums), custom_call_target="tpu_custom_call" | custom-call | tf_op jit(solution)/shard_map/store/pallas_call | solution.py:362

commit v4 on v3

--- a/solution.py
+++ b/solution.py
@@ -30,6 +30,16 @@
     def peer_of(p):
         return lax.rem(rep + 1 + p, reps)
 
+    cuts = sorted({0, chunk, min(2, pieces) * chunk, rows})
+
+    def slab_copy(i):
+        cols = pl.ds(cuts[i], cuts[i + 1] - cuts[i])
+        return pltpu.make_async_copy(master.at[:, cols], slab.at[:, cols], slab_sem.at[i])
+
+    slabs = len(cuts) - 1
+    for i in range(slabs):
+        slab_copy(i).start()
+
     barrier = pltpu.get_barrier_semaphore()
 
     @pl.when(has_left)
@@ -47,17 +57,8 @@
     for bit in bits:
         pl.semaphore_signal(barrier, inc=1, device_id={"tp": partner(bit)}, device_id_type=MESH)
 
-    cuts = sorted({0, chunk, min(2, pieces) * chunk, rows})
-
-    def slab_copy(i):
-        cols = pl.ds(cuts[i], cuts[i + 1] - cuts[i])
-        return pltpu.make_async_copy(master.at[:, cols], slab.at[:, cols], slab_sem.at[i])
-
-    slabs = len(cuts) - 1
     token_copy = pltpu.make_async_copy(probe, tokens, token_sem)
     bias_copy = pltpu.make_async_copy(bias, offset, bias_sem)
-    for i in range(slabs):
-        slab_copy(i).start()
     bias_copy.start()
     token_copy.start()
 
@@ -80,10 +81,11 @@
             device_id={"role": me + 2 * way - 1}, device_id_type=MESH,
         )
 
-    def share(r, g, p):
-        return pltpu.make_async_remote_copy(
-            src_ref=group(r, rep, g), dst_ref=group(r, rep, g),
-            send_sem=pass_sem.at[p], recv_sem=peer_sem.at[reps - 2 - p, r, g],
+    def share(r, k, p):
+        return pltpu.make_async_remote_copy(
+            src_ref=at(r, rep, k), dst_ref=at(r, rep, k),
+            send_sem=pass_sem.at[p],
+            recv_sem=peer_sem.at[reps - 2 - p, r, lax.div(k, pair)],
             device_id={"dp": peer_of(p)}, device_id_type=MESH,
         )
 
@@ -120,10 +122,9 @@
         def _():
             line(me, k, 1).start()
 
-        if k % pair == pair - 1:
-            @pl.loop(0, reps - 1)
-            def _(p):
-                share(me, k // pair, p).start()
+        @pl.loop(0, reps - 1)
+        def _(p):
+            share(me, jnp.int32(k), p).start()
 
     for k in range(pieces):
         if k < slabs:
@@ -218,11 +219,9 @@
                     def _():
                         line(r, k, way).start()
 
-                    @pl.when(whole)
-                    def _():
-                        @pl.loop(0, reps - 1)
-                        def _(p):
-                            share(r, g, p).start()
+                    @pl.loop(0, reps - 1)
+                    def _(p):
+                        share(r, k, p).start()
 
                     @pl.when(k == pieces - 1)
                     def _():

time: 43.5 us -> 43.4 us (level)
  no operation moved by 1% of the time
where the time goes in v4:
time: 43.4 us; the launch traced here: 43.2 us
  Pallas kernels  42.6 us (98%)
  between operations  0.64 us (1%)
    pallas_call x1, Pallas kernels, body(): pl.pallas_call(functools.partial(gather_kernel, n, reps, heads, rows, chu...  40.5 us
    pallas_call x1, Pallas kernels, body(): pl.pallas_call(store_kernel, out_shape=(jax.ShapeDtypeStruct(full.shape,...  2.13 us

profile of v4, /device:TPU:1, one launch (start us, length us, event | category | flops | bytes accessed | tf_op | source)
XLA Modules:
  0.0 43.2 jit_solution(7860958987425113732)
XLA Ops:
  0.6 40.5 %gather.1 = (bf16[8192,256]{1,0:T(8,128)(2,1)S(1)}, bf16[256,256]{1,0:T(8,128)(2,1)S(1)}, f32[8,8,128]{2,1,0:T(8,128)S(1)}) custom-call(f32[256,1024]{1,0:T(8,128)} %master.1, f32[1,256]{1,0:T(1,128)} %bitcast.2, bf16[256,8192]{1,0:T(8,128)(2,1)} %probe.1), custom_call_target="tpu_custom_call" | custom-call | tf_op jit(solution)/shard_map/gather/pallas_call | solution.py:322
  41.1 2.1 %store.1 = (bf16[8192,256]{1,0:T(8,128)(2,1)}, bf16[256,256]{1,0:T(8,128)(2,1)}, f32[8,8,128]{2,1,0:T(8,128)}) custom-call(bf16[8192,256]{1,0:T(8,128)(2,1)S(1)} %get-tuple-element.9.full, bf16[256,256]{1,0:T(8,128)(2,1)S(1)} %get-tuple-element.10.keys, f32[8,8,128]{2,1,0:T(8,128)S(1)} %get-tuple-element.11.sums), custom_call_target="tpu_custom_call" | custom-call | tf_op jit(solution)/shard_map/store/pallas_call | solution.py:361
